TPU v7x, 32 devices: a whole 2x2x4 slice. The times are simulated.
32 devices in a mesh: groups: 2 (over x), seq: 16 (over z, y, core).
Axes of the slice: x: 2, y: 2, z: 4, core: 2. Of those that a mesh axis runs over, the one named last changes fastest.
Arguments:
- activations: bfloat16 [512, 14336], P(('groups', 'seq')), parts along dimension 0, may hold values from -6 to 6
- out_grads: bfloat16 [512, 2048], P(('groups', 'seq')), parts along dimension 0, may hold values from -6 to 6
- query_ids: int32 [512], P(('groups', 'seq')), parts along dimension 0, may hold values from 0 to 2, never falling along the last dimension, each value on 1 to 128 neighbouring positions
- act_basis: bfloat16 [64, 224, 224], P('seq'), may hold values from -0.375 to 0.375
- grad_basis: bfloat16 [2048, 2048], P(None, 'seq'), may hold values from -0.125 to 0.125
- eigenvalues: float32 [2048, 14336], P(None, 'seq'), may hold values from 8 to 80
Outputs:
- precond: bfloat16 [6, 2048, 14336], P('groups', None, 'seq'), parts along dimension 0
There are 2 independent parts, one for each index of `groups`. A program takes and returns all parts, laid end to end along the dimension named above; an argument that names none is the same for every part. Nothing has to cross between parts.
Inputs may be any that keep to these rules, and one draw needn't show every extreme that they name: `query_ids`: query ids never fall along the tokens; each of the 3 queries has at least one and at most 128 tokens.
All inputs are finite; a program needn't handle non-finite values.
Results may differ from a plain program's by a relative error of at most 0.006.
Values may be sent and summed in bfloat16 or wider, within the bound.
A program may use at most 128 MiB of HBM per device.

v0:
```python
import jax
import jax.numpy as jnp
from jax import lax
from jax.sharding import PartitionSpec as P

QUERIES = 3


def shards(activations, out_grads, query_ids, act_basis, grad_basis, eigenvalues):
    local_blocks = act_basis.shape[0]
    block_order = act_basis.shape[1]
    out_units = grad_basis.shape[0]
    columns = lax.all_to_all(activations, "seq", split_axis=1, concat_axis=0, tiled=True)
    all_tokens = columns.shape[0]
    local_width = local_blocks * block_order
    rotated_act = jnp.einsum(
        "tbi,bik->tbk",
        columns.reshape(all_tokens, local_blocks, block_order),
        act_basis,
        preferred_element_type=jnp.float32,
    )
    rotated_act = rotated_act.astype(jnp.bfloat16).reshape(all_tokens, local_width)
    full_basis = lax.all_gather(grad_basis, "seq", axis=1, tiled=True)
    own_rotated = jnp.dot(out_grads, full_basis, preferred_element_type=jnp.float32).astype(
        jnp.bfloat16
    )
    rotated_grad, token_query = (
        lax.all_gather(own_rotated, "seq", axis=0, tiled=True),
        lax.all_gather(query_ids, "seq", axis=0, tiled=True),
    )
    selector = (token_query[:, None] == jnp.arange(QUERIES, dtype=jnp.int32)[None, :]).astype(
        jnp.bfloat16
    )
    selected = (rotated_act[:, None, :] * selector[:, :, None]).reshape(
        all_tokens, QUERIES * local_width
    )
    moments = lax.dot_general(
        rotated_grad, selected, (((0,), (0,)), ((), ())), preferred_element_type=jnp.float32
    )
    scaled = (moments.reshape(out_units, QUERIES, local_width) / eigenvalues[:, None, :]).astype(
        jnp.bfloat16
    )
    rotated_back = jnp.einsum(
        "dqbk,bik->dqbi",
        scaled.reshape(out_units, QUERIES, local_blocks, block_order),
        act_basis,
        preferred_element_type=jnp.float32,
    )
    rotated_back = rotated_back.astype(jnp.bfloat16).reshape(out_units, QUERIES * local_width)
    result = jnp.dot(full_basis, rotated_back, preferred_element_type=jnp.float32)
    result = result.reshape(out_units, QUERIES, local_width)
    return jnp.transpose(result, (1, 0, 2)).astype(jnp.bfloat16)


def solution(mesh):
    return jax.shard_map(
        shards,
        mesh=mesh,
        in_specs=(
            P(("groups", "seq"), None),
            P(("groups", "seq"), None),
            P(("groups", "seq")),
            P("seq", None, None),
            P(None, "seq"),
            P(None, "seq"),
        ),
        out_specs=P("groups", None, "seq"),
        check_vma=False,
    )
```

profile of v0, /device:TPU:0, one launch (start us, length us, event | category | flops | bytes accessed | tf_op | source)
XLA Modules:
  0.0 207.3 jit_solution(7658103903438815733)
XLA Ops:
  6.5 0.0 copy-start
  6.5 0.0 copy-start.2
  6.5 0.0 all-gather.3.cloned.1.call-start
  6.5 0.7 all-gather.3.cloned.1.call-update
  7.3 0.0 all-gather.5.cloned.1.call-start
  7.3 82.6 %all-gather.3.cloned.1.call-done = bf16[2048,2048]{1,0:T(8,128)(2,1)} async-done(((bf16[2048,128]{1,0:T(8,128)(2,1)}), bf16[2048,2048]{1,0:T(8,128)(2,1)}) %all-gather.3.cloned.1.call-update) | async-done | bytes 8388624 | tf_op jit(solution)/shard_map/all_gather | solution.py:23
  90.0 5.2 %convolution_convert_fusion.1 = bf16[16,2048]{1,0:T(8,128)(2,1)} fusion(bf16[16,2048]{1,0:T(8,128)(2,1)} %param.7, bf16[2048,2048]{1,0:T(8,128)(2,1)} %all-gather.3.cloned.1.call-done), kind=kOutput, calls=%fused_computation.5 | convolution fusion | flops 134250496 | bytes 8519680 | tf_op jit(solution)/shard_map/dot_general | solution.py:24
  95.2 0.0 copy-start.4
  95.2 0.0 copy-start.3
  95.2 0.0 all-gather.5.cloned.1.call-update
  95.2 0.0 copy-done.2
  95.2 0.8 copy.29
  96.0 3.6 %all-to-all-start = ((bf16[16,16,896]{2,0,1:T(8,128)(2,1)}), bf16[16,16,896]{2,0,1:T(8,128)(2,1)S(1)}, u32[]{:S(2)}, u32[]{:S(2)}) async-start(bf16[16,16,896]{2,0,1:T(8,128)(2,1)} %bitcast.36), calls=%async_computation | async-start | bytes 917504 | tf_op jit(solution)/shard_map/all_to_all | solution.py:13
  99.6 8.6 %copy.15 = f32[2048,896]{0,1:T(8,128)} copy(f32[2048,896]{1,0:T(8,128)} %param.11) | data formatting | bytes 14680064 | tf_op args[5]
  108.2 0.0 copy-done.4
  108.2 0.6 dynamic-slice
  109.4 0.0 copy-done.3
  109.4 0.2 dynamic-update-slice
  109.6 12.4 %all-reduce = s32[256]{0:T(256)S(1)} all-reduce(s32[256]{0:T(256)S(1)} %dynamic-update-slice), channel_id=1, replica_groups=mesh['groups'=2,'seq'=16] {'seq'}, use_global_device_ids=true, to_apply=%add | all-reduce | flops 256 | bytes 2048
  122.1 0.0 all-to-all-done
  122.1 0.5 reshape.45
  122.6 0.0 copy-done
  122.6 0.3 convolution_convert_fusion.2
  122.9 10.5 %all-gather.5.cloned.1.call-done = bf16[256,2048]{1,0:T(8,128)(2,1)} async-done(((bf16[16,2048]{1,0:T(8,128)(2,1)}), bf16[256,2048]{1,0:T(8,128)(2,1)}) %all-gather.5.cloned.1.call-update) | async-done | bytes 1048592 | tf_op jit(solution)/shard_map/all_gather | solution.py:28
  133.5 8.2 %divide_convert_fusion = bf16[2048,3,896]{0,2,1:T(8,128)(2,1)} fusion(f32[2048,896]{0,1:T(8,128)} %copy.15, bf16[256,2048]{1,0:T(8,128)(2,1)} %all-gather.5.cloned.1.call-done, bf16[256,3]{0,1:T(4,128)(2,1)S(1)} %fusion.11, bf16[256,896]{0,1:T(8,128)(2,1)S(1)} %bitcast.42), kind=kOutput, calls=%fused_computation | convolution fusion | flops 2832334848 | bytes 19858944 | tf_op jit(solution)/shard_map/dot_general | solution.py:37
  141.6 11.3 %convert_bitcast_fusion = bf16[2048,3,4,224]{0,3,1,2:T(8,128)(2,1)} fusion(bf16[2048,3,4,224]{0,3,2,1:T(8,128)(2,1)} %bitcast.37, bf16[4,224,224]{2,1,0:T(8,128)(2,1)S(1)} %copy-done), kind=kOutput, calls=%fused_computation.4 | convolution fusion | flops 2471755776 | bytes 22421504 | tf_op jit(solution)/shard_map/dqbk,bik->dqbi/dot_general | solution.py:43
  153.0 5.8 %copy.17 = bf16[2048,3,4,224]{0,3,2,1:T(8,128)(2,1)S(1)} copy(bf16[2048,3,4,224]{0,3,1,2:T(8,128)(2,1)} %convert_bitcast_fusion) | data formatting | bytes 22020096 | tf_op jit(solution)/shard_map/convert_element_type | solution.py:49
  158.8 27.0 %convolution_convert_fusion = bf16[2688,2048]{1,0:T(8,128)(2,1)} fusion(bf16[2048,2688]{0,1:T(8,128)(2,1)S(1)} %bitcast.38, bf16[2048,2048]{1,0:T(8,128)(2,1)} %all-gather.3.cloned.1.call-done), kind=kOutput, calls=%fused_computation.1 | convolution fusion | flops 22554083328 | bytes 30408704 | tf_op jit(solution)/shard_map/dot_general | solution.py:50
  185.8 0.0 copy-start.1
  185.8 14.7 %copy.18 = bf16[2048,3,896]{2,0,1:T(8,128)(2,1)} copy(bf16[2048,3,896]{0,2,1:T(8,128)(2,1)} %bitcast.39) | data formatting | bytes 22020096 | tf_op jit(solution)/shard_map/convert_element_type | solution.py:52
  200.5 0.0 copy-done.1
  (2 shorter events, 0.0 us)
Async XLA Ops:
  6.5 116.0 %copy-start = (bf16[4,224,224]{2,1,0:T(8,128)(2,1)S(1)}, bf16[4,224,224]{2,1,0:T(8,128)(2,1)}, u32[]{:S(2)}) copy-start(bf16[4,224,224]{2,1,0:T(8,128)(2,1)} %param.9) | copy-start | bytes 1204228
  6.5 88.7 %copy-start.2 = (bf16[16,14336]{1,0:T(8,128)(2,1)S(1)}, bf16[16,14336]{1,0:T(8,128)(2,1)}, u32[]{:S(2)}) copy-start(bf16[16,14336]{1,0:T(8,128)(2,1)} %param.6) | copy-start | bytes 1376260
  6.5 83.4 %all-gather.3.cloned.1.call-start = ((), (), s32[]{:S(2)}) async-start(), calls=%async_computation.1 | async-start | bytes 8912896 | tf_op jit(solution)/shard_map/all_gather | solution.py:23
  7.3 126.2 %all-gather.5.cloned.1.call-start = ((), (), s32[]{:S(2)}) async-start(), calls=%async_computation.2 | async-start | bytes 1114112 | tf_op jit(solution)/shard_map/all_gather | solution.py:28
  95.2 13.0 %copy-start.4 = (u32[32]{0:T(128)S(1)}, u32[32]{0:T(128)}, u32[]{:S(2)}) copy-start(u32[32]{0:T(128)} %constant.6) | copy-start | bytes 388
  95.2 14.2 %copy-start.3 = (s32[16]{0:T(128)S(1)}, s32[16]{0:T(128)}, u32[]{:S(2)}) copy-start(s32[16]{0:T(128)} %param.8) | copy-start | bytes 196
  96.0 26.0 %all-to-all-start = ((bf16[16,16,896]{2,0,1:T(8,128)(2,1)}), bf16[16,16,896]{2,0,1:T(8,128)(2,1)S(1)}, u32[]{:S(2)}, u32[]{:S(2)}) async-start(bf16[16,16,896]{2,0,1:T(8,128)(2,1)} %bitcast.36), calls=%async_computation | async-start | bytes 917504 | tf_op jit(solution)/shard_map/all_to_all | solution.py:13
  185.8 14.7 %copy-start.1 = (bf16[4,224,224]{2,1,0:T(8,128)(2,1)S(1)}, bf16[4,224,224]{2,1,0:T(8,128)(2,1)}, u32[]{:S(2)}) copy-start(bf16[4,224,224]{2,1,0:T(8,128)(2,1)} %param.9) | copy-start | bytes 1204228
Sparse Core Ops, SparseCore 0:
  9.5 80.4 all-gather.2
  95.3 38.0 all-gather.4
where the time goes:
time: 208 us; the launch traced here: 207 us
  waiting for transfers between devices  93.9 us (45%)
  matrix products  52.1 us (25%)
  local copies, waits for them, and re-layouts  31.2 us (15%)
  between operations  14 us (7%)
  blocking collectives  12.4 us (6%)
  starting transfers between devices  3.6 us (2%)
    all_gather x1, waiting for transfers between devices, shards(): full_basis = lax.all_gather(grad_basis, 'seq', axis=1, tiled=True)  82.6 us
    dot_general x1, matrix products, shards(): jnp.dot(full_basis, rotated_back, preferred_element_type=jnp.float32)  27 us
    convert_element_type x1, local copies, waits for them, and re-layouts, shards(): return jnp.transpose(result, (1, 0, 2)).astype(jnp.bfloat16)  14.7 us
    unnamed x1, blocking collectives  12.4 us
    dot_general x1, matrix products, shards(): jnp.einsum('dqbk,bik->dqbi', scaled.reshape(out_units, QUERIES, local_blo...  11.3 us
    all_gather x1, waiting for transfers between devices, shards(): lax.all_gather(own_rotated, 'seq', axis=0, tiled=True)  10.5 us
    unnamed x14, local copies, waits for them, and re-layouts  9.46 us
    dot_general x1, matrix products, shards(): lax.dot_general(rotated_grad, selected, (((0,), (0,)), ((), ())), preferr...  8.18 us
  transfers between devices with their start and end apart: 3, of which 2 were waited for; matrix products, arithmetic and copies ran while one was open for 5% of the time, Pallas kernels for 0%

commit v1 on v0

--- a/solution.py
+++ b/solution.py
@@ -20,7 +20,14 @@
         preferred_element_type=jnp.float32,
     )
     rotated_act = rotated_act.astype(jnp.bfloat16).reshape(all_tokens, local_width)
-    full_basis = lax.all_gather(grad_basis, "seq", axis=1, tiled=True)
+
+    def run_words(chip_axis, x_part):
+        mixed_arr = lax.psum(1, chip_axis)
+        frame_out = jnp.stack(mixed_arr * [x_part])
+        block_now = lax.all_to_all(frame_out, chip_axis, 0, 0)
+        return jnp.concatenate(block_now, 1)
+
+    full_basis = run_words("seq", grad_basis)
     own_rotated = jnp.dot(out_grads, full_basis, preferred_element_type=jnp.float32).astype(
         jnp.bfloat16
     )

time: 208 us -> 321 us (1.54)
  blocking collectives: 12.4 us -> 202 us
  waiting for transfers between devices: 93.9 us -> 10.8 us
  local copies, waits for them, and re-layouts: 31.2 us -> 37 us
    all_to_all x0 -> x1, blocking collectives: none -> 189 us  [run_words(): block_now = lax.all_to_all(frame_out, chip_axis, 0, 0)]
    all_gather x1 -> x0, waiting for transfers between devices: 82.6 us -> none  [shards(): full_basis = lax.all_gather(grad_basis, 'seq', axis=1, tiled=True)]
    unnamed x14 -> x19, local copies, waits for them, and re-layouts: 9.46 us -> 14.2 us
  transfers between devices with their start and end apart: 3 -> 2, of which waited for: 2 -> 1; matrix products, arithmetic and copies ran while one was open for 5% -> 3% of each run, Pallas kernels for 0% -> 0%
where the time goes in v1:
time: 321 us; the launch traced here: 320 us
  blocking collectives  202 us (63%)
  matrix products  51 us (16%)
  local copies, waits for them, and re-layouts  37 us (12%)
  between operations  14.1 us (4%)
  waiting for transfers between devices  10.8 us (3%)
  starting transfers between devices  5.72 us (2%)
    all_to_all x1, blocking collectives, run_words(): block_now = lax.all_to_all(frame_out, chip_axis, 0, 0)  189 us
    dot_general x1, matrix products, shards(): jnp.dot(full_basis, rotated_back, preferred_element_type=jnp.float32)  28.2 us
    convert_element_type x1, local copies, waits for them, and re-layouts, shards(): return jnp.transpose(result, (1, 0, 2)).astype(jnp.bfloat16)  14.7 us
    unnamed x19, local copies, waits for them, and re-layouts  14.2 us
    unnamed x1, blocking collectives  12.5 us
    dot_general x1, matrix products, shards(): jnp.einsum('dqbk,bik->dqbi', scaled.reshape(out_units, QUERIES, local_blo...  11.4 us
    all_gather x1, waiting for transfers between devices, shards(): lax.all_gather(own_rotated, 'seq', axis=0, tiled=True)  10.8 us
    dot_general x1, matrix products, shards(): lax.dot_general(rotated_grad, selected, (((0,), (0,)), ((), ())), preferr...  8.18 us
  transfers between devices with their start and end apart: 2, of which 1 were waited for; matrix products, arithmetic and copies ran while one was open for 3% of the time, Pallas kernels for 0%

profile of v1, /device:TPU:0, one launch (start us, length us, event | category | flops | bytes accessed | tf_op | source)
XLA Modules:
  0.0 320.5 jit_solution(4088509647162580671)
XLA Ops:
  6.5 0.0 copy-start
  6.5 0.0 all-gather.2.cloned.1.call-start
  6.5 1.3 copy.12
  7.8 0.0 copy-start.4
  7.9 1.1 stack.2
  8.9 0.0 copy-start.3
  8.9 189.3 %all_to_all.21 = bf16[16,2048,128]{1,2,0:T(8,128)(2,1)S(1)} all-to-all(bf16[16,2048,128]{1,2,0:T(8,128)(2,1)S(1)} %stack.2), channel_id=1, replica_groups=mesh['groups'=2,'seq'=16] {'seq'}, dimensions={0} | all-to-all | bytes 16777216 | tf_op jit(solution)/shard_map/all_to_all | solution.py:27
  198.3 0.0 copy-start.2
  198.3 3.3 %copy-done.2 = bf16[16,2048,128]{1,2,0:T(8,128)(2,1)} copy-done((bf16[16,2048,128]{1,2,0:T(8,128)(2,1)}, bf16[16,2048,128]{1,2,0:T(8,128)(2,1)S(1)}, u32[]{:S(2)}) %copy-start.2) | copy-done | bytes 8388632
  201.6 0.0 copy-done.4
  201.6 2.9 convolution_convert_fusion.1
  204.5 0.0 all-gather.2.cloned.1.call-update
  204.5 0.0 copy-done.3
  204.5 0.8 copy.30
  205.3 5.7 %all-to-all-start.1 = ((bf16[16,16,896]{2,0,1:T(8,128)(2,1)}), bf16[16,16,896]{2,0,1:T(8,128)(2,1)S(1)}, u32[]{:S(2)}, u32[]{:S(2)}) async-start(bf16[16,16,896]{2,0,1:T(8,128)(2,1)} %bitcast.39), calls=%async_computation.1 | async-start | bytes 917504 | tf_op jit(solution)/shard_map/all_to_all | solution.py:13
  211.0 8.7 %copy.16 = f32[2048,896]{0,1:T(8,128)} copy(f32[2048,896]{1,0:T(8,128)} %param.11) | data formatting | bytes 14680064 | tf_op args[5]
  219.7 0.0 copy-done.6
  219.7 0.6 dynamic-slice
  221.0 0.0 copy-done.5
  221.0 0.2 dynamic-update-slice
  221.3 12.5 %all-reduce = s32[256]{0:T(256)S(1)} all-reduce(s32[256]{0:T(256)S(1)} %dynamic-update-slice), channel_id=1, replica_groups=mesh['groups'=2,'seq'=16] {'seq'}, use_global_device_ids=true, to_apply=%add | all-reduce | flops 256 | bytes 2048
  233.7 0.0 all-to-all-done.1
  233.7 0.5 reshape.55
  234.2 0.0 copy-done
  234.2 0.3 convolution_convert_fusion.2
  234.6 10.8 %all-gather.2.cloned.1.call-done = bf16[256,2048]{1,0:T(8,128)(2,1)} async-done(((bf16[16,2048]{1,0:T(8,128)(2,1)}), bf16[256,2048]{1,0:T(8,128)(2,1)}) %all-gather.2.cloned.1.call-update) | async-done | bytes 1048592 | tf_op jit(solution)/shard_map/all_gather | solution.py:35
  245.4 8.2 %divide_convert_fusion = bf16[2048,3,896]{0,2,1:T(8,128)(2,1)} fusion(f32[2048,896]{0,1:T(8,128)} %copy.16, bf16[256,2048]{1,0:T(8,128)(2,1)} %all-gather.2.cloned.1.call-done, bf16[256,3]{0,1:T(4,128)(2,1)S(1)} %fusion.11, bf16[256,896]{0,1:T(8,128)(2,1)S(1)} %bitcast.47), kind=kOutput, calls=%fused_computation | convolution fusion | flops 2832334848 | bytes 19858944 | tf_op jit(solution)/shard_map/dot_general | solution.py:44
  253.6 11.4 %convert_bitcast_fusion = bf16[2048,3,4,224]{0,3,1,2:T(8,128)(2,1)} fusion(bf16[2048,3,4,224]{0,3,2,1:T(8,128)(2,1)} %bitcast.42, bf16[4,224,224]{2,1,0:T(8,128)(2,1)S(1)} %copy-done), kind=kOutput, calls=%fused_computation.4 | convolution fusion | flops 2471755776 | bytes 22421504 | tf_op jit(solution)/shard_map/dqbk,bik->dqbi/dot_general | solution.py:50
  264.9 5.8 %copy.18 = bf16[2048,3,4,224]{0,3,2,1:T(8,128)(2,1)S(1)} copy(bf16[2048,3,4,224]{0,3,1,2:T(8,128)(2,1)} %convert_bitcast_fusion) | data formatting | bytes 22020096 | tf_op jit(solution)/shard_map/convert_element_type | solution.py:56
  270.7 28.2 %convolution_convert_fusion = bf16[2688,2048]{1,0:T(8,128)(2,1)} fusion(bf16[2048,2688]{0,1:T(8,128)(2,1)S(1)} %bitcast.43, bf16[2048,2048]{0,1:T(8,128)(2,1)} %bitcast.41), kind=kOutput, calls=%fused_computation.1 | convolution fusion | flops 22554083328 | bytes 30408704 | tf_op jit(solution)/shard_map/dot_general | solution.py:57
  298.9 14.7 %copy.19 = bf16[2048,3,896]{2,0,1:T(8,128)(2,1)} copy(bf16[2048,3,896]{0,2,1:T(8,128)(2,1)} %bitcast.44) | data formatting | bytes 22020096 | tf_op jit(solution)/shard_map/convert_element_type | solution.py:59
  313.6 0.0 copy-done.1
  (5 shorter events, 0.0 us)
Async XLA Ops:
  6.5 227.7 %copy-start = (bf16[4,224,224]{2,1,0:T(8,128)(2,1)S(1)}, bf16[4,224,224]{2,1,0:T(8,128)(2,1)}, u32[]{:S(2)}) copy-start(bf16[4,224,224]{2,1,0:T(8,128)(2,1)} %param.9) | copy-start | bytes 1204228
  6.5 238.8 %all-gather.2.cloned.1.call-start = ((), (), s32[]{:S(2)}) async-start(), calls=%async_computation.2 | async-start | bytes 1114112 | tf_op jit(solution)/shard_map/all_gather | solution.py:35
  7.8 193.7 %copy-start.4 = (bf16[16,2048]{1,0:T(8,128)(2,1)S(1)}, bf16[16,2048]{1,0:T(8,128)(2,1)}, u32[]{:S(2)}) copy-start(bf16[16,2048]{1,0:T(8,128)(2,1)} %param.7) | copy-start | bytes 196612
  8.9 195.6 %copy-start.3 = (bf16[16,14336]{1,0:T(8,128)(2,1)S(1)}, bf16[16,14336]{1,0:T(8,128)(2,1)}, u32[]{:S(2)}) copy-start(bf16[16,14336]{1,0:T(8,128)(2,1)} %param.6) | copy-start | bytes 1376260
  198.3 3.3 %copy-start.2 = (bf16[16,2048,128]{1,2,0:T(8,128)(2,1)}, bf16[16,2048,128]{1,2,0:T(8,128)(2,1)S(1)}, u32[]{:S(2)}) copy-start(bf16[16,2048,128]{1,2,0:T(8,128)(2,1)S(1)} %all_to_all.21) | copy-start | bytes 25165828
  201.6 18.1 %copy-start.6 = (u32[32]{0:T(128)S(1)}, u32[32]{0:T(128)}, u32[]{:S(2)}) copy-start(u32[32]{0:T(128)} %constant.6) | copy-start | bytes 388
  201.6 19.4 %copy-start.5 = (s32[16]{0:T(128)S(1)}, s32[16]{0:T(128)}, u32[]{:S(2)}) copy-start(s32[16]{0:T(128)} %param.8) | copy-start | bytes 196
  205.3 28.4 %all-to-all-start.1 = ((bf16[16,16,896]{2,0,1:T(8,128)(2,1)}), bf16[16,16,896]{2,0,1:T(8,128)(2,1)S(1)}, u32[]{:S(2)}, u32[]{:S(2)}) async-start(bf16[16,16,896]{2,0,1:T(8,128)(2,1)} %bitcast.39), calls=%async_computation.1 | async-start | bytes 917504 | tf_op jit(solution)/shard_map/all_to_all | solution.py:13
  298.9 14.7 %copy-start.1 = (bf16[4,224,224]{2,1,0:T(8,128)(2,1)S(1)}, bf16[4,224,224]{2,1,0:T(8,128)(2,1)}, u32[]{:S(2)}) copy-start(bf16[4,224,224]{2,1,0:T(8,128)(2,1)} %param.9) | copy-start | bytes 1204228
Sparse Core Ops, SparseCore 0:
  204.6 40.7 all-gather.1
